TPU v7x, 32 devices: a whole 2x2x4 slice. The times are simulated.
32 devices in a mesh: rows: 8 (over z, y), cols: 4 (over x, core).
Axes of the slice: x: 2, y: 2, z: 4, core: 2. Of those that a mesh axis runs over, the one named last changes fastest.
Arguments:
- orthophoto: float32 [3, 1024, 2048], P(None, 'rows', 'cols'), may hold values from 0 to 1
Outputs:
- detail_zero: float32 [3, 1024, 2048], P(None, 'rows', 'cols')
- detail_one: float32 [3, 512, 1024], P(None, 'rows', 'cols')
- detail_two: float32 [3, 256, 512], P(None, 'rows', 'cols')
- detail_three: float32 [3, 128, 256], P(None, 'rows', 'cols')
- detail_four: float32 [3, 64, 128], P(None, 'rows', 'cols')
- coarsest: float32 [3, 32, 64], P(None, 'rows', 'cols')
All inputs are finite; a program needn't handle non-finite values.
Results may differ from a plain program's by a relative error of at most 0.00015.
Values sent between devices are 32-bit elements; how exact they have to be, the bound alone decides.
A program may use at most 64 MiB of HBM per device.

v0:
```python
import functools

import jax
import jax.numpy as jnp
from jax import lax
from jax.experimental import pallas as pl
from jax.experimental.pallas import tpu as pltpu
from jax.sharding import PartitionSpec as P

LEVELS = 5
LANES = 128
EDGE = 8
ABOVE, BELOW = 24, 16
BF16 = jnp.bfloat16
F32 = jnp.float32
MESH = pl.DeviceIdType.MESH
DIRECTIONS = ((-1, 0), (1, 0), (0, -1), (0, 1), (-1, -1), (-1, 1), (1, -1), (1, 1))


def pitch(width):
    return width + LANES if width >= LANES else LANES


def local_of(lane, width, total):
    return jnp.where(lane < width + (total - width) // 2, lane, lane - total)


def reduce_tap(distance):
    far = jnp.abs(distance)
    return jnp.where(far == 0, 0.375, jnp.where(far == 1, 0.25, jnp.where(far == 2, 0.0625, 0.0)))


def expand_tap(distance):
    far = jnp.abs(distance)
    return jnp.where(far == 0, 0.75, jnp.where(far == 1, 0.5, jnp.where(far == 2, 0.125, 0.0)))


def fill_weights(ref, col, in_width, in_cols, out_width, out_halo, expanding):
    in_total, out_total = ref.shape
    chunk = 32

    def one(step, carry):
        base = step * chunk
        lane_in = base + lax.broadcasted_iota(jnp.int32, (chunk, out_total), 0)
        lane_out = lax.broadcasted_iota(jnp.int32, (chunk, out_total), 1)
        g = local_of(lane_in, in_width, in_total) + col * in_width
        if out_halo:
            lane_out = local_of(lane_out, out_width, out_total)
        j = lane_out + col * out_width
        if expanding:
            w = expand_tap(2 * g - j)
            w = w + jnp.where(g >= 1, expand_tap(-2 * g - j), 0.0)
            w = w + expand_tap(2 * (2 * in_cols - 1 - g) - j)
        else:
            w = reduce_tap(g - 2 * j)
            w = w + jnp.where(g >= 1, reduce_tap(-g - 2 * j), 0.0)
            w = w + jnp.where(g <= in_cols - 2, reduce_tap(2 * (in_cols - 1) - g - 2 * j), 0.0)
        w = jnp.where((g >= 0) & (g < in_cols), w, 0.0)
        ref[pl.ds(pl.multiple_of(base, chunk), chunk), :] = w.astype(BF16)
        return carry

    lax.fori_loop(0, in_total // chunk, one, 0)


def product(values, weights):
    high = values.astype(BF16)
    rest = values - high.astype(F32)
    middle = rest.astype(BF16)
    low = (rest - middle.astype(F32)).astype(BF16)
    out = jnp.dot(low, weights, preferred_element_type=F32)
    out = out + jnp.dot(middle, weights, preferred_element_type=F32)
    return out + jnp.dot(high, weights, preferred_element_type=F32)


def strided(ref, channel, start, count):
    tiles = ref.shape[1]
    return [ref[channel, t, pl.ds(start, count, stride=2), :] for t in range(tiles)]


def kernel(
    image_cols, x_hbm, d0_hbm, d1_ref, d2_ref, d3_ref, d4_ref, c_ref,
    x, send_l, send_r, got_l, got_r, corner,
    v1, l1, l2own, l2, l2side, v3, l3, v4, l4, v5, l5, exp_buf, d0,
    w1, w2, w3, w4, w5, e1, e2, e3, e4, e5,
    local_sem, send_a, recv_a, send_b, recv_b,
):
    channels, rows, width = x_hbm.shape
    row, col = lax.axis_index("rows"), lax.axis_index("cols")
    last_row, last_col = lax.axis_size("rows") - 1, lax.axis_size("cols") - 1
    top, bottom, left, right = row == 0, row == last_row, col == 0, col == last_col
    tiles = width // LANES

    def exists(direction):
        dr, dc = direction
        ok = None
        for flag in ([top] if dr < 0 else [bottom] if dr > 0 else []) + ([left] if dc < 0 else [right] if dc > 0 else []):
            ok = jnp.logical_not(flag) if ok is None else jnp.logical_and(ok, jnp.logical_not(flag))
        return ok

    takes = [
        pltpu.make_async_copy(
            x_hbm.at[:, :, pl.ds(t * LANES, LANES)], x.at[:, t, pl.ds(EDGE, rows), :], local_sem.at[t]
        )
        for t in range(tiles)
    ]
    for take in takes:
        take.start()

    barrier = pltpu.get_barrier_semaphore()
    for direction in DIRECTIONS:
        @pl.when(exists(direction))
        def _(direction=direction):
            pl.semaphore_signal(
                barrier, inc=1, device_id=(row + direction[0], col + direction[1]), device_id_type=MESH
            )

    widths = [width >> k for k in range(LEVELS + 1)]
    cols = [image_cols >> k for k in range(LEVELS + 1)]
    fill_weights(w1, col, widths[0], cols[0], widths[1], True, False)

    for take in takes:
        take.wait()
    for ch in range(channels):
        send_l[ch] = x[ch, 0, pl.ds(EDGE, rows), :].T[:EDGE]
        send_r[ch] = x[ch, tiles - 1, pl.ds(EDGE, rows), :].T[LANES - EDGE:]

    tall = 3 - jnp.where(top, 1, 0) - jnp.where(bottom, 1, 0)
    broad = 3 - jnp.where(left, 1, 0) - jnp.where(right, 1, 0)
    pl.semaphore_wait(barrier, tall * broad - 1)

    def copy_a(number):
        dr, dc = DIRECTIONS[number]
        if dc == 0:
            src = x.at[:, pl.ds(0, tiles), pl.ds(EDGE, EDGE) if dr < 0 else pl.ds(rows, EDGE), :]
            dst = x.at[:, pl.ds(0, tiles), pl.ds(rows + EDGE, EDGE) if dr < 0 else pl.ds(0, EDGE), :]
        elif dr == 0:
            src, dst = (send_l, got_r) if dc < 0 else (send_r, got_l)
        else:
            src = x.at[:, 0 if dc < 0 else tiles - 1, pl.ds(EDGE, EDGE) if dr < 0 else pl.ds(rows, EDGE), :]
            dst = corner.at[number - 4]
        return pltpu.make_async_remote_copy(
            src_ref=src, dst_ref=dst, send_sem=send_a.at[number], recv_sem=recv_a.at[number],
            device_id=(row + dr, col + dc), device_id_type=MESH,
        )

    rows2 = rows // 4

    def copy_b(number):
        dr, dc = DIRECTIONS[number]
        if dr < 0:
            src_rows, dst_rows = pl.ds(0, BELOW), pl.ds(ABOVE + rows2, BELOW)
        elif dr > 0:
            src_rows, dst_rows = pl.ds(rows2 - ABOVE, ABOVE), pl.ds(0, ABOVE)
        else:
            src_rows, dst_rows = pl.ds(0, rows2), pl.ds(ABOVE, rows2)
        dst = l2.at[:, 0, dst_rows, :] if dc == 0 else l2side.at[0 if dc > 0 else 1, :, dst_rows, :]
        return pltpu.make_async_remote_copy(
            src_ref=l2own.at[:, src_rows, :], dst_ref=dst, send_sem=send_b.at[number], recv_sem=recv_b.at[number],
            device_id=(row + dr, col + dc), device_id_type=MESH,
        )

    def each(copy, opposite, act):
        for number, (dr, dc) in enumerate(DIRECTIONS):
            @pl.when(exists((-dr, -dc) if opposite else (dr, dc)))
            def _(number=number):
                act(copy(number))

    each(copy_a, False, lambda c: c.start())
    fill_weights(w2, col, widths[1], cols[1], widths[2], False, False)
    fill_weights(e1, col, widths[1], cols[1], widths[0], False, True)
    each(copy_a, True, lambda c: c.wait_recv())

    lane = lax.broadcasted_iota(jnp.int32, (EDGE, LANES), 1)
    on_right = lane < LANES // 2
    for ch in range(channels):
        gap = jnp.zeros((LANES - 2 * EDGE, rows), F32)
        from_right = jnp.where(right, 0.0, got_r[ch])
        from_left = jnp.where(left, 0.0, got_l[ch])
        x[ch, tiles, pl.ds(EDGE, rows), :] = jnp.concatenate([from_right, gap, from_left], axis=0).T
        for above in (True, False):
            low = corner[3 if above else 1, ch]
            high = corner[2 if above else 0, ch]
            mixed = jnp.where(on_right, jnp.where(right, 0.0, high), jnp.where(left, 0.0, low))
            x[ch, tiles, pl.ds(0 if above else rows + EDGE, EDGE), :] = mixed

    def at_ends(ref, first, own, reducing):
        lead = (slice(None),) * (len(ref.shape) - 2)

        @pl.when(top)
        def _():
            ref[lead + (pl.ds(first - 1, 1),)] = ref[lead + (pl.ds(first + 1, 1),)]
            if reducing:
                ref[lead + (pl.ds(first - 2, 1),)] = ref[lead + (pl.ds(first + 2, 1),)]

        @pl.when(bottom)
        def _():
            ref[lead + (pl.ds(first + own, 1),)] = ref[lead + (pl.ds(first + own - (2 if reducing else 1), 1),)]

    def reduce_rows(src, dst, start, count):
        for ch in range(channels):
            for t in range(src.shape[1]):
                part = [src[ch, t, pl.ds(start + k, count, stride=2), :] for k in range(5)]
                total = (part[0] + part[4]) * 0.0625 + (part[1] + part[3]) * 0.25 + part[2] * 0.375
                dst[ch, pl.ds(0, count), pl.ds(t * LANES, LANES)] = total

    def reduce_cols(src, weights, dst):
        depth = src.shape[1]
        out = product(src[...].reshape(channels * depth, src.shape[2]), weights[...])
        for ch in range(channels):
            for t in range(dst.shape[1]):
                dst[ch, t] = out[ch * depth:(ch + 1) * depth, t * LANES:(t + 1) * LANES]

    def residual(fine, fine_first, coarse, first, own, weights, out, out_width):
        at_ends(coarse, first, own, False)
        depth = coarse.shape[2]
        flat = jnp.concatenate(
            [coarse[:, t].reshape(channels * depth, LANES) for t in range(coarse.shape[1])], axis=1
        )
        wide = product(flat, weights[...])
        out_tiles = weights.shape[1] // LANES
        for t in range(out_tiles):
            exp_buf[pl.ds(0, channels * depth), :] = wide[:, t * LANES:(t + 1) * LANES]
            for ch in range(channels):
                at = ch * depth + first
                before = exp_buf[pl.ds(at - 1, own), :]
                center = exp_buf[pl.ds(at, own), :]
                after = exp_buf[pl.ds(at + 1, own), :]
                even = fine[ch, t, pl.ds(fine_first, own, stride=2), :] - (before + 6.0 * center + after) * 0.125
                odd = fine[ch, t, pl.ds(fine_first + 1, own, stride=2), :] - (center + after) * 0.5
                d0[ch, t, pl.ds(0, own, stride=2), :] = even
                d0[ch, t, pl.ds(1, own, stride=2), :] = odd
        if out is not None:
            for ch in range(channels):
                for t in range(out_tiles):
                    lanes = min(LANES, out_width)
                    out[ch, :, pl.ds(t * LANES, lanes)] = d0[ch, t, pl.ds(0, 2 * own), :][:, :lanes]

    at_ends(x, EDGE, rows, True)
    first1 = (EDGE - 2) // 2
    count1 = (x.shape[2] - 3 - EDGE) // 2 + first1 + 1
    reduce_rows(x, v1, EDGE - 2 - 2 * first1, count1)
    reduce_cols(v1, w1, l1)
    at_ends(l1, first1, rows // 2, True)
    reduce_rows(l1, v5, first1 - 2, rows2)
    own = product(
        v5[:, pl.ds(0, rows2), :].reshape(channels * rows2, v5.shape[2]), w2[...]
    )
    for ch in range(channels):
        l2own[ch] = own[ch * rows2:(ch + 1) * rows2]
        l2[ch, 0, pl.ds(ABOVE, rows2), :] = own[ch * rows2:(ch + 1) * rows2]
    each(copy_b, False, lambda c: c.start())

    residual(x, EDGE, l1, first1, rows // 2, e1, None, width)
    puts = [
        pltpu.make_async_copy(d0.at[:, t], d0_hbm.at[:, :, pl.ds(t * LANES, LANES)], local_sem.at[t])
        for t in range(tiles)
    ]
    for put in puts:
        put.start()
    fill_weights(w3, col, widths[2], cols[2], widths[3], True, False)
    fill_weights(e2, col, widths[2], cols[2], widths[1], False, True)
    fill_weights(w4, col, widths[3], cols[3], widths[4], True, False)
    fill_weights(w5, col, widths[4], cols[4], widths[5], True, False)
    fill_weights(e3, col, widths[3], cols[3], widths[2], False, True)
    fill_weights(e4, col, widths[4], cols[4], widths[3], False, True)
    fill_weights(e5, col, widths[5], cols[5], widths[4], False, True)
    each(copy_b, True, lambda c: c.wait_recv())

    lane = lax.broadcasted_iota(jnp.int32, (l2.shape[2], LANES), 1)
    for ch in range(channels):
        l2[ch, 1] = jnp.where(
            lane < LANES // 2,
            jnp.where(right, 0.0, l2side[1, ch]),
            jnp.where(left, 0.0, l2side[0, ch]),
        )

    for put in puts:
        put.wait()

    firsts = [EDGE, first1, ABOVE]
    counts = [None, None, l2.shape[2]]
    residual(l1, first1, l2, ABOVE, rows2, e2, d1_ref, widths[1])
    level, fine = l2, l2
    owns = [rows >> k for k in range(LEVELS + 1)]
    stages = ((v3, w3, l3, e3, d2_ref), (v4, w4, l4, e4, d3_ref), (None, w5, l5, e5, d4_ref))
    for k, (v, w, coarse, e, out) in enumerate(stages, start=2):
        if v is None:
            v = v4
        at_ends(level, firsts[k], owns[k], True)
        first = (firsts[k] - 2) // 2
        count = (counts[k] - 3 - firsts[k]) // 2 + first + 1
        depth = -(-count // 8) * 8
        firsts.append(first)
        counts.append(count)
        for ch in range(channels):
            for t in range(level.shape[1]):
                part = [level[ch, t, pl.ds(firsts[k] - 2 - 2 * first + i, count, stride=2), :] for i in range(5)]
                total = (part[0] + part[4]) * 0.0625 + (part[1] + part[3]) * 0.25 + part[2] * 0.375
                v[ch, pl.ds(0, count), pl.ds(t * LANES, LANES)] = total
        made = product(v[:, pl.ds(0, depth), :].reshape(channels * depth, v.shape[2]), w[...])
        for ch in range(channels):
            coarse[ch, 0] = made[ch * depth:(ch + 1) * depth]
        residual(level, firsts[k], coarse, first, owns[k + 1], e, out, widths[k])
        level = coarse
    for ch in range(channels):
        c_ref[ch] = l5[ch, 0, pl.ds(firsts[5], owns[5]), :][:, :widths[5]]

    each(copy_a, False, lambda c: c.wait_send())
    each(copy_b, False, lambda c: c.wait_send())


def solution(mesh):
    def body(x):
        channels, rows, width = x.shape
        image_cols = width * mesh.shape["cols"]
        widths = [width >> k for k in range(LEVELS + 1)]
        p = [pitch(w) for w in widths]
        vm = lambda *shape: pltpu.VMEM(shape, F32)
        wt = lambda *shape: pltpu.VMEM(shape, BF16)
        rows2 = rows // 4
        ext = ABOVE + rows2 + BELOW
        up8 = lambda n: -(-n // 8) * 8
        n1 = up8(rows // 2 + EDGE - 2)
        f3, n3 = (ABOVE - 2) // 2, (ext - 3 - ABOVE) // 2 + (ABOVE - 2) // 2 + 1
        f4, n4 = (f3 - 2) // 2, (n3 - 3 - f3) // 2 + (f3 - 2) // 2 + 1
        n5 = (n4 - 3 - f4) // 2 + (f4 - 2) // 2 + 1
        shape = lambda k: jax.ShapeDtypeStruct((channels, rows >> k, width >> k), F32)
        vmem = pl.BlockSpec(memory_space=pltpu.VMEM)
        anywhere = pl.BlockSpec(memory_space=pl.ANY)
        return pl.pallas_call(
            functools.partial(kernel, image_cols),
            out_shape=tuple(shape(k) for k in range(LEVELS + 1)),
            in_specs=[anywhere],
            out_specs=(anywhere,) + (vmem,) * LEVELS,
            scratch_shapes=[
                vm(channels, p[0] // LANES, rows + 2 * EDGE, LANES),
                vm(channels, EDGE, rows), vm(channels, EDGE, rows),
                vm(channels, EDGE, rows), vm(channels, EDGE, rows),
                vm(4, channels, EDGE, LANES),
                vm(channels, n1, p[0]),
                vm(channels, p[1] // LANES, n1, LANES),
                vm(channels, rows2, LANES),
                vm(channels, p[2] // LANES, ext, LANES),
                vm(2, channels, ext, LANES),
                vm(channels, up8(n3), p[2]),
                vm(channels, 1, up8(n3), LANES),
                vm(channels, up8(n4), p[3]),
                vm(channels, 1, up8(n4), LANES),
                vm(channels, rows2, p[1]),
                vm(channels, 1, up8(n5), LANES),
                vm(channels * max(n1, ext) + 8, LANES),
                vm(channels, width // LANES, rows, LANES),
                wt(p[0], p[1]), wt(p[1], widths[2]), wt(p[2], p[3]), wt(p[3], p[4]), wt(p[4], p[5]),
                wt(p[1], widths[0]), wt(p[2], widths[1]), wt(p[3], LANES), wt(p[4], LANES), wt(p[5], LANES),
                pltpu.SemaphoreType.DMA((width // LANES,)),
                pltpu.SemaphoreType.DMA((8,)), pltpu.SemaphoreType.DMA((8,)),
                pltpu.SemaphoreType.DMA((8,)), pltpu.SemaphoreType.DMA((8,)),
            ],
            compiler_params=pltpu.CompilerParams(collective_id=0, has_side_effects=True),
            name="pyramid",
        )(x)

    placed = P(None, "rows", "cols")
    return jax.shard_map(
        body, mesh=mesh, in_specs=(placed,), out_specs=(placed,) * (LEVELS + 1), check_vma=False
    )
```

profile of v0, /device:TPU:21, one launch (start us, length us, event | category | flops | bytes accessed | tf_op | source)
XLA Modules:
  0.0 22.3 jit_solution(1797290422344689129)
XLA Ops:
  0.6 16.0 %pyramid.1 = (f32[3,128,512]{2,1,0:T(8,128)}, f32[3,64,256]{2,1,0:T(8,128)}, f32[3,32,128]{2,1,0:T(8,128)}, f32[3,16,64]{2,1,0:T(8,128)}, f32[3,8,32]{2,1,0:T(8,128)}, /*index=5*/f32[3,4,16]{2,1,0:T(4,128)}) custom-call(f32[3,128,512]{2,1,0:T(8,128)} %x_hbm.1), custom_call_target="tpu_custom_call" | custom-call | tf_op jit(solution)/shard_map/pyramid/pallas_call | solution.py:330
  16.6 0.0 copy-start
  16.6 2.1 %copy.13 = f32[3,128,512]{2,1,0:T(8,128)} copy(f32[3,128,512]{2,1,0:T(8,128)} %get-tuple-element.12) | data formatting | bytes 1572864
  18.7 0.0 copy-done
  18.7 0.0 copy-start.1
  18.7 0.7 %copy.14 = f32[3,64,256]{2,1,0:T(8,128)} copy(f32[3,64,256]{2,1,0:T(8,128)S(1)} %copy-done) | data formatting | bytes 393216
  19.4 0.1 copy-done.1
  19.5 0.0 copy-start.2
  19.5 0.6 %copy.15 = f32[3,32,128]{2,1,0:T(8,128)} copy(f32[3,32,128]{2,1,0:T(8,128)S(1)} %copy-done.1) | data formatting | bytes 98304
  20.1 0.1 copy-done.2
  20.2 0.0 copy-start.3
  20.2 0.6 %copy.16 = f32[3,16,64]{2,1,0:T(8,128)} copy(f32[3,16,64]{2,1,0:T(8,128)S(1)} %copy-done.2) | data formatting | bytes 24576
  20.9 0.1 copy-done.3
  21.0 0.0 copy-start.4
  21.0 0.6 %copy.17 = f32[3,8,32]{2,1,0:T(8,128)} copy(f32[3,8,32]{2,1,0:T(8,128)S(1)} %copy-done.3) | data formatting | bytes 6144
  21.6 0.1 copy-done.4
  21.7 0.6 %copy.18 = f32[3,4,16]{2,1,0:T(4,128)} copy(f32[3,4,16]{2,1,0:T(4,128)S(1)} %copy-done.4) | data formatting | bytes 1536
Async XLA Ops:
  16.6 2.1 %copy-start = (f32[3,64,256]{2,1,0:T(8,128)S(1)}, f32[3,64,256]{2,1,0:T(8,128)}, u32[]{:S(2)}) copy-start(f32[3,64,256]{2,1,0:T(8,128)} %get-tuple-element.13) | copy-start | bytes 589828
  18.7 0.8 %copy-start.1 = (f32[3,32,128]{2,1,0:T(8,128)S(1)}, f32[3,32,128]{2,1,0:T(8,128)}, u32[]{:S(2)}) copy-start(f32[3,32,128]{2,1,0:T(8,128)} %get-tuple-element.14) | copy-start | bytes 147460
  19.5 0.7 %copy-start.2 = (f32[3,16,64]{2,1,0:T(8,128)S(1)}, f32[3,16,64]{2,1,0:T(8,128)}, u32[]{:S(2)}) copy-start(f32[3,16,64]{2,1,0:T(8,128)} %get-tuple-element.15) | copy-start | bytes 36868
  20.2 0.7 %copy-start.3 = (f32[3,8,32]{2,1,0:T(8,128)S(1)}, f32[3,8,32]{2,1,0:T(8,128)}, u32[]{:S(2)}) copy-start(f32[3,8,32]{2,1,0:T(8,128)} %get-tuple-element.16) | copy-start | bytes 9220
  21.0 0.7 %copy-start.4 = (f32[3,4,16]{2,1,0:T(4,128)S(1)}, f32[3,4,16]{2,1,0:T(4,128)}, u32[]{:S(2)}) copy-start(f32[3,4,16]{2,1,0:T(4,128)} %get-tuple-element.17) | copy-start | bytes 2308
where the time goes:
time: 22.6 us; the launch traced here: 22.3 us
  Pallas kernels  16 us (71%)
  local copies, waits for them, and re-layouts  5.65 us (25%)
  between operations  0.65 us (3%)
    pallas_call x1, Pallas kernels, body(): pl.pallas_call(functools.partial(kernel, image_cols), out_shape=tuple((sh...  16 us
    unnamed x16, local copies, waits for them, and re-layouts  5.65 us

commit v1 on v0

--- a/solution.py
+++ b/solution.py
@@ -11,6 +11,7 @@
 LANES = 128
 EDGE = 8
 ABOVE, BELOW = 24, 16
+VMEM_GRANT = 24 << 20
 BF16 = jnp.bfloat16
 F32 = jnp.float32
 MESH = pl.DeviceIdType.MESH
@@ -72,15 +73,27 @@
     return out + jnp.dot(high, weights, preferred_element_type=F32)
 
 
-def strided(ref, channel, start, count):
-    tiles = ref.shape[1]
-    return [ref[channel, t, pl.ds(start, count, stride=2), :] for t in range(tiles)]
+def hand_out(first5, d0, d1, d2, d3, d4, l5, d0_hbm, d1_hbm, d2_hbm, d3_out, d4_out, c_out, sem):
+    puts = []
+    for src, dst in ((d0, d0_hbm), (d1, d1_hbm), (d2, d2_hbm)):
+        for t in range(src.shape[1]):
+            puts.append(
+                pltpu.make_async_copy(src.at[:, t], dst.at[:, :, pl.ds(t * LANES, LANES)], sem.at[len(puts)])
+            )
+    for put in puts:
+        put.start()
+    for ch in range(d3_out.shape[0]):
+        d3_out[ch] = d3[ch, 0][:, :d3_out.shape[2]]
+        d4_out[ch] = d4[ch, 0][:, :d4_out.shape[2]]
+        c_out[ch] = l5[ch, 0, pl.ds(first5, c_out.shape[1]), :][:, :c_out.shape[2]]
+    for put in puts:
+        put.wait()
 
 
 def kernel(
-    image_cols, x_hbm, d0_hbm, d1_ref, d2_ref, d3_ref, d4_ref, c_ref,
+    image_cols, x_hbm, d0, d1, d2, d3, d4, l5,
     x, send_l, send_r, got_l, got_r, corner,
-    v1, l1, l2own, l2, l2side, v3, l3, v4, l4, v5, l5, exp_buf, d0,
+    v1, l1, l2own, l2, l2side, v3, l3, v4, l4, v5, v2, exp0, exp1, exp2, exp3, exp4,
     w1, w2, w3, w4, w5, e1, e2, e3, e4, e5,
     local_sem, send_a, recv_a, send_b, recv_b,
 ):
@@ -186,15 +199,14 @@
     def at_ends(ref, first, own, reducing):
         lead = (slice(None),) * (len(ref.shape) - 2)
 
-        @pl.when(top)
-        def _():
-            ref[lead + (pl.ds(first - 1, 1),)] = ref[lead + (pl.ds(first + 1, 1),)]
-            if reducing:
-                ref[lead + (pl.ds(first - 2, 1),)] = ref[lead + (pl.ds(first + 2, 1),)]
-
-        @pl.when(bottom)
-        def _():
-            ref[lead + (pl.ds(first + own, 1),)] = ref[lead + (pl.ds(first + own - (2 if reducing else 1), 1),)]
+        def fix(flag, to, source):
+            to, source = lead + (pl.ds(to, 1),), lead + (pl.ds(source, 1),)
+            ref[to] = jnp.where(flag, ref[source], ref[to])
+
+        fix(top, first - 1, first + 1)
+        if reducing:
+            fix(top, first - 2, first + 2)
+        fix(bottom, first + own, first + own - (2 if reducing else 1))
 
     def reduce_rows(src, dst, start, count):
         for ch in range(channels):
@@ -210,30 +222,24 @@
             for t in range(dst.shape[1]):
                 dst[ch, t] = out[ch * depth:(ch + 1) * depth, t * LANES:(t + 1) * LANES]
 
-    def residual(fine, fine_first, coarse, first, own, weights, out, out_width):
+    def residual(fine, fine_first, coarse, first, own, weights, buffer, out):
         at_ends(coarse, first, own, False)
         depth = coarse.shape[2]
         flat = jnp.concatenate(
             [coarse[:, t].reshape(channels * depth, LANES) for t in range(coarse.shape[1])], axis=1
         )
         wide = product(flat, weights[...])
-        out_tiles = weights.shape[1] // LANES
-        for t in range(out_tiles):
-            exp_buf[pl.ds(0, channels * depth), :] = wide[:, t * LANES:(t + 1) * LANES]
+        for t in range(out.shape[1]):
+            buffer[t] = wide[:, t * LANES:(t + 1) * LANES]
             for ch in range(channels):
                 at = ch * depth + first
-                before = exp_buf[pl.ds(at - 1, own), :]
-                center = exp_buf[pl.ds(at, own), :]
-                after = exp_buf[pl.ds(at + 1, own), :]
+                before = buffer[t, pl.ds(at - 1, own), :]
+                center = buffer[t, pl.ds(at, own), :]
+                after = buffer[t, pl.ds(at + 1, own), :]
                 even = fine[ch, t, pl.ds(fine_first, own, stride=2), :] - (before + 6.0 * center + after) * 0.125
                 odd = fine[ch, t, pl.ds(fine_first + 1, own, stride=2), :] - (center + after) * 0.5
-                d0[ch, t, pl.ds(0, own, stride=2), :] = even
-                d0[ch, t, pl.ds(1, own, stride=2), :] = odd
-        if out is not None:
-            for ch in range(channels):
-                for t in range(out_tiles):
-                    lanes = min(LANES, out_width)
-                    out[ch, :, pl.ds(t * LANES, lanes)] = d0[ch, t, pl.ds(0, 2 * own), :][:, :lanes]
+                out[ch, t, pl.ds(0, own, stride=2), :] = even
+                out[ch, t, pl.ds(1, own, stride=2), :] = odd
 
     at_ends(x, EDGE, rows, True)
     first1 = (EDGE - 2) // 2
@@ -241,22 +247,16 @@
     reduce_rows(x, v1, EDGE - 2 - 2 * first1, count1)
     reduce_cols(v1, w1, l1)
     at_ends(l1, first1, rows // 2, True)
-    reduce_rows(l1, v5, first1 - 2, rows2)
+    reduce_rows(l1, v2, first1 - 2, rows2)
     own = product(
-        v5[:, pl.ds(0, rows2), :].reshape(channels * rows2, v5.shape[2]), w2[...]
+        v2[...].reshape(channels * rows2, v2.shape[2]), w2[...]
     )
     for ch in range(channels):
         l2own[ch] = own[ch * rows2:(ch + 1) * rows2]
         l2[ch, 0, pl.ds(ABOVE, rows2), :] = own[ch * rows2:(ch + 1) * rows2]
     each(copy_b, False, lambda c: c.start())
 
-    residual(x, EDGE, l1, first1, rows // 2, e1, None, width)
-    puts = [
-        pltpu.make_async_copy(d0.at[:, t], d0_hbm.at[:, :, pl.ds(t * LANES, LANES)], local_sem.at[t])
-        for t in range(tiles)
-    ]
-    for put in puts:
-        put.start()
+    residual(x, EDGE, l1, first1, rows // 2, e1, exp0, d0)
     fill_weights(w3, col, widths[2], cols[2], widths[3], True, False)
     fill_weights(e2, col, widths[2], cols[2], widths[1], False, True)
     fill_weights(w4, col, widths[3], cols[3], widths[4], True, False)
@@ -274,18 +274,13 @@
             jnp.where(left, 0.0, l2side[0, ch]),
         )
 
-    for put in puts:
-        put.wait()
-
     firsts = [EDGE, first1, ABOVE]
     counts = [None, None, l2.shape[2]]
-    residual(l1, first1, l2, ABOVE, rows2, e2, d1_ref, widths[1])
-    level, fine = l2, l2
+    residual(l1, first1, l2, ABOVE, rows2, e2, exp1, d1)
+    level = l2
     owns = [rows >> k for k in range(LEVELS + 1)]
-    stages = ((v3, w3, l3, e3, d2_ref), (v4, w4, l4, e4, d3_ref), (None, w5, l5, e5, d4_ref))
-    for k, (v, w, coarse, e, out) in enumerate(stages, start=2):
-        if v is None:
-            v = v4
+    stages = ((v3, w3, l3, e3, exp2, d2), (v4, w4, l4, e4, exp3, d3), (v5, w5, l5, e5, exp4, d4))
+    for k, (v, w, coarse, e, buffer, out) in enumerate(stages, start=2):
         at_ends(level, firsts[k], owns[k], True)
         first = (firsts[k] - 2) // 2
         count = (counts[k] - 3 - firsts[k]) // 2 + first + 1
@@ -300,11 +295,8 @@
         made = product(v[:, pl.ds(0, depth), :].reshape(channels * depth, v.shape[2]), w[...])
         for ch in range(channels):
             coarse[ch, 0] = made[ch * depth:(ch + 1) * depth]
-        residual(level, firsts[k], coarse, first, owns[k + 1], e, out, widths[k])
+        residual(level, firsts[k], coarse, first, owns[k + 1], e, buffer, out)
         level = coarse
-    for ch in range(channels):
-        c_ref[ch] = l5[ch, 0, pl.ds(firsts[5], owns[5]), :][:, :widths[5]]
-
     each(copy_a, False, lambda c: c.wait_send())
     each(copy_b, False, lambda c: c.wait_send())
 
@@ -324,14 +316,18 @@
         f3, n3 = (ABOVE - 2) // 2, (ext - 3 - ABOVE) // 2 + (ABOVE - 2) // 2 + 1
         f4, n4 = (f3 - 2) // 2, (n3 - 3 - f3) // 2 + (f3 - 2) // 2 + 1
         n5 = (n4 - 3 - f4) // 2 + (f4 - 2) // 2 + 1
+        f5 = (f4 - 2) // 2
         shape = lambda k: jax.ShapeDtypeStruct((channels, rows >> k, width >> k), F32)
+        tiled = [(channels, max(widths[k] // LANES, 1), rows >> k, LANES) for k in range(LEVELS)]
+        tiled.append((channels, 1, up8(n5), LANES))
+        depths = [n1, ext, up8(n3), up8(n4), up8(n5)]
         vmem = pl.BlockSpec(memory_space=pltpu.VMEM)
         anywhere = pl.BlockSpec(memory_space=pl.ANY)
-        return pl.pallas_call(
+        held = pl.pallas_call(
             functools.partial(kernel, image_cols),
-            out_shape=tuple(shape(k) for k in range(LEVELS + 1)),
+            out_shape=tuple(vm(*dims) for dims in tiled),
             in_specs=[anywhere],
-            out_specs=(anywhere,) + (vmem,) * LEVELS,
+            out_specs=(vmem,) * (LEVELS + 1),
             scratch_shapes=[
                 vm(channels, p[0] // LANES, rows + 2 * EDGE, LANES),
                 vm(channels, EDGE, rows), vm(channels, EDGE, rows),
@@ -346,19 +342,30 @@
                 vm(channels, 1, up8(n3), LANES),
                 vm(channels, up8(n4), p[3]),
                 vm(channels, 1, up8(n4), LANES),
+                vm(channels, up8(n5), p[4]),
                 vm(channels, rows2, p[1]),
-                vm(channels, 1, up8(n5), LANES),
-                vm(channels * max(n1, ext) + 8, LANES),
-                vm(channels, width // LANES, rows, LANES),
+                *(vm(tiled[k][1], channels * depths[k], LANES) for k in range(LEVELS)),
                 wt(p[0], p[1]), wt(p[1], widths[2]), wt(p[2], p[3]), wt(p[3], p[4]), wt(p[4], p[5]),
                 wt(p[1], widths[0]), wt(p[2], widths[1]), wt(p[3], LANES), wt(p[4], LANES), wt(p[5], LANES),
                 pltpu.SemaphoreType.DMA((width // LANES,)),
                 pltpu.SemaphoreType.DMA((8,)), pltpu.SemaphoreType.DMA((8,)),
                 pltpu.SemaphoreType.DMA((8,)), pltpu.SemaphoreType.DMA((8,)),
             ],
-            compiler_params=pltpu.CompilerParams(collective_id=0, has_side_effects=True),
+            compiler_params=pltpu.CompilerParams(
+                collective_id=0, has_side_effects=True, vmem_limit_bytes=VMEM_GRANT
+            ),
             name="pyramid",
         )(x)
+        copies = sum(dims[1] for dims in tiled[:3])
+        return pl.pallas_call(
+            functools.partial(hand_out, f5),
+            out_shape=tuple(shape(k) for k in range(LEVELS + 1)),
+            in_specs=[anywhere] * 3 + [vmem] * 3,
+            out_specs=(anywhere,) * 3 + (vmem,) * 3,
+            scratch_shapes=[pltpu.SemaphoreType.DMA((copies,))],
+            compiler_params=pltpu.CompilerParams(vmem_limit_bytes=VMEM_GRANT),
+            name="hand_out",
+        )(*(pltpu.with_memory_space_constraint(part, pltpu.VMEM) for part in held))
 
     placed = P(None, "rows", "cols")
     return jax.shard_map(

time: 22.6 us -> 18.1 us (0.80); the launches traced: 22.3 us -> 18 us
  local copies, waits for them, and re-layouts: 5.65 us -> 1.13 us
    unnamed x16 -> x2, local copies, waits for them, and re-layouts: 5.65 us -> 1.13 us
    pallas_call x1 -> x2, Pallas kernels: 16 us -> 16.2 us  [the longest x1 14.6 us: body(): pl.pallas_call(functools.partial(kernel, image_cols), out_shape=tuple((vm...]
where the time goes in v1:
time: 18.1 us; the launch traced here: 18 us
  Pallas kernels  16.2 us (90%)
  local copies, waits for them, and re-layouts  1.13 us (6%)
  between operations  0.65 us (4%)
    pallas_call x1, Pallas kernels, body(): pl.pallas_call(functools.partial(kernel, image_cols), out_shape=tuple((vm...  14.6 us
    pallas_call x1, Pallas kernels, body(): pl.pallas_call(functools.partial(hand_out, f5), out_shape=tuple((shape(k)...  1.62 us
    unnamed x2, local copies, waits for them, and re-layouts  1.13 us

profile of v1, /device:TPU:21, one launch (start us, length us, event | category | flops | bytes accessed | tf_op | source)
XLA Modules:
  0.0 18.0 jit_solution(4048753432761876268)
XLA Ops:
  0.6 0.0 copy-start
  0.6 1.1 %copy-done = f32[3,128,512]{2,1,0:T(8,128)S(1)} copy-done((f32[3,128,512]{2,1,0:T(8,128)S(1)}, f32[3,128,512]{2,1,0:T(8,128)}, u32[]{:S(2)}) %copy-start) | copy-done | bytes 786456
  1.8 14.6 %pyramid.1 = (f32[3,4,128,128]{3,2,1,0:T(8,128)S(1)}, f32[3,2,64,128]{3,2,1,0:T(8,128)S(1)}, f32[3,1,32,128]{3,2,1,0:T(8,128)S(1)}, f32[3,1,16,128]{3,2,1,0:T(8,...) custom-call(f32[3,128,512]{2,1,0:T(8,128)S(1)} %copy-done), custom_call_target="tpu_custom_call" | custom-call | tf_op jit(solution)/shard_map/pyramid/pallas_call | solution.py:326
  16.4 1.6 %hand_out.1 = (f32[3,128,512]{2,1,0:T(8,128)}, f32[3,64,256]{2,1,0:T(8,128)}, f32[3,32,128]{2,1,0:T(8,128)}, f32[3,16,64]{2,1,0:T(8,128)}, f32[3,8,32]{2,1,0:T(8,128)}, /*index=5*/f32[3,4,16]{2,1,0:T(4,128)}) custom-call(f32[3,4,128,128]{3,2,1,0:T(8,128)S(1)} %get-tuple-element.12.d0, f32[3,2,64,128]{3,2,1,0:T(8,128)S(1)} %get-tuple-element.13.d1, ...), custom_call_target="tpu_custom_call" | custom-call | tf_op jit(solution)/shard_map/hand_out/pallas_call | solution.py:360
Async XLA Ops:
  0.6 1.1 %copy-start = (f32[3,128,512]{2,1,0:T(8,128)S(1)}, f32[3,128,512]{2,1,0:T(8,128)}, u32[]{:S(2)}) copy-start(f32[3,128,512]{2,1,0:T(8,128)} %x_hbm.1) | copy-start | bytes 2359300

commit v2 on v1

--- a/solution.py
+++ b/solution.py
@@ -93,7 +93,7 @@
 def kernel(
     image_cols, x_hbm, d0, d1, d2, d3, d4, l5,
     x, send_l, send_r, got_l, got_r, corner,
-    v1, l1, l2own, l2, l2side, v3, l3, v4, l4, v5, v2, exp0, exp1, exp2, exp3, exp4,
+    v1, l1, l2own, l2, side_l, side_r, side_got_l, side_got_r, v3, l3, v4, l4, v5, v2, exp0, exp1, exp2, exp3, exp4,
     w1, w2, w3, w4, w5, e1, e2, e3, e4, e5,
     local_sem, send_a, recv_a, send_b, recv_b,
 ):
@@ -166,9 +166,14 @@
             src_rows, dst_rows = pl.ds(rows2 - ABOVE, ABOVE), pl.ds(0, ABOVE)
         else:
             src_rows, dst_rows = pl.ds(0, rows2), pl.ds(ABOVE, rows2)
-        dst = l2.at[:, 0, dst_rows, :] if dc == 0 else l2side.at[0 if dc > 0 else 1, :, dst_rows, :]
+        if dc == 0:
+            src, dst = l2own.at[:, src_rows, :], l2.at[:, 0, dst_rows, :]
+        elif dc < 0:
+            src, dst = side_l, side_got_r.at[1 - dr]
+        else:
+            src, dst = side_r, side_got_l.at[1 - dr]
         return pltpu.make_async_remote_copy(
-            src_ref=l2own.at[:, src_rows, :], dst_ref=dst, send_sem=send_b.at[number], recv_sem=recv_b.at[number],
+            src_ref=src, dst_ref=dst, send_sem=send_b.at[number], recv_sem=recv_b.at[number],
             device_id=(row + dr, col + dc), device_id_type=MESH,
         )
 
@@ -181,21 +186,6 @@
     each(copy_a, False, lambda c: c.start())
     fill_weights(w2, col, widths[1], cols[1], widths[2], False, False)
     fill_weights(e1, col, widths[1], cols[1], widths[0], False, True)
-    each(copy_a, True, lambda c: c.wait_recv())
-
-    lane = lax.broadcasted_iota(jnp.int32, (EDGE, LANES), 1)
-    on_right = lane < LANES // 2
-    for ch in range(channels):
-        gap = jnp.zeros((LANES - 2 * EDGE, rows), F32)
-        from_right = jnp.where(right, 0.0, got_r[ch])
-        from_left = jnp.where(left, 0.0, got_l[ch])
-        x[ch, tiles, pl.ds(EDGE, rows), :] = jnp.concatenate([from_right, gap, from_left], axis=0).T
-        for above in (True, False):
-            low = corner[3 if above else 1, ch]
-            high = corner[2 if above else 0, ch]
-            mixed = jnp.where(on_right, jnp.where(right, 0.0, high), jnp.where(left, 0.0, low))
-            x[ch, tiles, pl.ds(0 if above else rows + EDGE, EDGE), :] = mixed
-
     def at_ends(ref, first, own, reducing):
         lead = (slice(None),) * (len(ref.shape) - 2)
 
@@ -208,19 +198,12 @@
             fix(top, first - 2, first + 2)
         fix(bottom, first + own, first + own - (2 if reducing else 1))
 
-    def reduce_rows(src, dst, start, count):
+    def reduce_rows(src, dst, start, count, at=0, lane_tiles=None):
         for ch in range(channels):
-            for t in range(src.shape[1]):
-                part = [src[ch, t, pl.ds(start + k, count, stride=2), :] for k in range(5)]
+            for t in range(src.shape[1]) if lane_tiles is None else lane_tiles:
+                part = [src[ch, t, pl.ds(start + 2 * at + k, count, stride=2), :] for k in range(5)]
                 total = (part[0] + part[4]) * 0.0625 + (part[1] + part[3]) * 0.25 + part[2] * 0.375
-                dst[ch, pl.ds(0, count), pl.ds(t * LANES, LANES)] = total
-
-    def reduce_cols(src, weights, dst):
-        depth = src.shape[1]
-        out = product(src[...].reshape(channels * depth, src.shape[2]), weights[...])
-        for ch in range(channels):
-            for t in range(dst.shape[1]):
-                dst[ch, t] = out[ch * depth:(ch + 1) * depth, t * LANES:(t + 1) * LANES]
+                dst[ch, pl.ds(at, count), pl.ds(t * LANES, LANES)] = total
 
     def residual(fine, fine_first, coarse, first, own, weights, buffer, out):
         at_ends(coarse, first, own, False)
@@ -241,11 +224,49 @@
                 out[ch, t, pl.ds(0, own, stride=2), :] = even
                 out[ch, t, pl.ds(1, own, stride=2), :] = odd
 
-    at_ends(x, EDGE, rows, True)
     first1 = (EDGE - 2) // 2
     count1 = (x.shape[2] - 3 - EDGE) // 2 + first1 + 1
-    reduce_rows(x, v1, EDGE - 2 - 2 * first1, count1)
-    reduce_cols(v1, w1, l1)
+    start1 = EDGE - 2 - 2 * first1
+    inner, inner_end, depth1 = 8, rows // 2, v1.shape[1]
+    height = inner_end - inner
+    reduce_rows(x, v1, start1, height, inner, range(tiles))
+    main = product(
+        v1[:, pl.ds(inner, height), pl.ds(0, width)].reshape(channels * height, width), w1[pl.ds(0, width), :]
+    )
+    for ch in range(channels):
+        for t in range(l1.shape[1]):
+            l1[ch, t, pl.ds(inner, height), :] = main[ch * height:(ch + 1) * height, t * LANES:(t + 1) * LANES]
+    each(copy_a, True, lambda c: c.wait_recv())
+
+    lane = lax.broadcasted_iota(jnp.int32, (EDGE, LANES), 1)
+    on_right = lane < LANES // 2
+    for ch in range(channels):
+        gap = jnp.zeros((LANES - 2 * EDGE, rows), F32)
+        from_right = jnp.where(right, 0.0, got_r[ch])
+        from_left = jnp.where(left, 0.0, got_l[ch])
+        x[ch, tiles, pl.ds(EDGE, rows), :] = jnp.concatenate([from_right, gap, from_left], axis=0).T
+        for above in (True, False):
+            low = corner[3 if above else 1, ch]
+            high = corner[2 if above else 0, ch]
+            mixed = jnp.where(on_right, jnp.where(right, 0.0, high), jnp.where(left, 0.0, low))
+            x[ch, tiles, pl.ds(0 if above else rows + EDGE, EDGE), :] = mixed
+
+    at_ends(x, EDGE, rows, True)
+    reduce_rows(x, v1, start1, inner, 0, range(tiles))
+    reduce_rows(x, v1, start1, count1 - inner_end, inner_end, range(tiles))
+    reduce_rows(x, v1, start1, count1, 0, (tiles,))
+    rim = depth1 - height
+    outer = jnp.concatenate([v1[:, pl.ds(0, inner), :], v1[:, pl.ds(inner_end, depth1 - inner_end), :]], axis=1)
+    outer = product(outer.reshape(channels * rim, v1.shape[2]), w1[...])
+    share = product(
+        v1[:, pl.ds(inner, height), pl.ds(width, LANES)].reshape(channels * height, LANES), w1[pl.ds(width, LANES), :]
+    )
+    for ch in range(channels):
+        for t in range(l1.shape[1]):
+            lanes = slice(t * LANES, (t + 1) * LANES)
+            l1[ch, t, pl.ds(0, inner), :] = outer[ch * rim:ch * rim + inner, lanes]
+            l1[ch, t, pl.ds(inner_end, depth1 - inner_end), :] = outer[ch * rim + inner:(ch + 1) * rim, lanes]
+            l1[ch, t, pl.ds(inner, height), :] += share[ch * height:(ch + 1) * height, lanes]
     at_ends(l1, first1, rows // 2, True)
     reduce_rows(l1, v2, first1 - 2, rows2)
     own = product(
@@ -254,6 +275,11 @@
     for ch in range(channels):
         l2own[ch] = own[ch * rows2:(ch + 1) * rows2]
         l2[ch, 0, pl.ds(ABOVE, rows2), :] = own[ch * rows2:(ch + 1) * rows2]
+    packed = side_l.shape[1]
+    filler = jnp.zeros((packed - channels * rows2, LANES), F32)
+    flipped = jnp.concatenate([own, filler], axis=0).T
+    side_l[...] = flipped[:BELOW]
+    side_r[...] = flipped[LANES - ABOVE:]
     each(copy_b, False, lambda c: c.start())
 
     residual(x, EDGE, l1, first1, rows // 2, e1, exp0, d0)
@@ -266,13 +292,15 @@
     fill_weights(e5, col, widths[5], cols[5], widths[4], False, True)
     each(copy_b, True, lambda c: c.wait_recv())
 
-    lane = lax.broadcasted_iota(jnp.int32, (l2.shape[2], LANES), 1)
-    for ch in range(channels):
-        l2[ch, 1] = jnp.where(
-            lane < LANES // 2,
-            jnp.where(right, 0.0, l2side[1, ch]),
-            jnp.where(left, 0.0, l2side[0, ch]),
-        )
+    gap = jnp.zeros((LANES - ABOVE - BELOW, packed), F32)
+    parts = ((rows2 - ABOVE, ABOVE, 0), (0, rows2, ABOVE), (0, BELOW, ABOVE + rows2))
+    for slot, (take_from, take_count, put_at) in enumerate(parts):
+        from_right = jnp.where(right, 0.0, side_got_r[slot])
+        from_left = jnp.where(left, 0.0, side_got_l[slot])
+        block = jnp.concatenate([from_right, gap, from_left], axis=0).T
+        for ch in range(channels):
+            at = ch * rows2 + take_from
+            l2[ch, 1, pl.ds(put_at, take_count), :] = block[at:at + take_count]
 
     firsts = [EDGE, first1, ABOVE]
     counts = [None, None, l2.shape[2]]
@@ -311,6 +339,7 @@
         wt = lambda *shape: pltpu.VMEM(shape, BF16)
         rows2 = rows // 4
         ext = ABOVE + rows2 + BELOW
+        packed = -(-channels * rows2 // LANES) * LANES
         up8 = lambda n: -(-n // 8) * 8
         n1 = up8(rows // 2 + EDGE - 2)
         f3, n3 = (ABOVE - 2) // 2, (ext - 3 - ABOVE) // 2 + (ABOVE - 2) // 2 + 1
@@ -326,7 +355,7 @@
         held = pl.pallas_call(
             functools.partial(kernel, image_cols),
             out_shape=tuple(vm(*dims) for dims in tiled),
-            in_specs=[anywhere],
+            in_specs=[pl.BlockSpec(memory_space=pltpu.HBM)],
             out_specs=(vmem,) * (LEVELS + 1),
             scratch_shapes=[
                 vm(channels, p[0] // LANES, rows + 2 * EDGE, LANES),
@@ -337,7 +366,7 @@
                 vm(channels, p[1] // LANES, n1, LANES),
                 vm(channels, rows2, LANES),
                 vm(channels, p[2] // LANES, ext, LANES),
-                vm(2, channels, ext, LANES),
+                vm(BELOW, packed), vm(ABOVE, packed), vm(3, ABOVE, packed), vm(3, BELOW, packed),
                 vm(channels, up8(n3), p[2]),
                 vm(channels, 1, up8(n3), LANES),
                 vm(channels, up8(n4), p[3]),
@@ -351,9 +380,7 @@
                 pltpu.SemaphoreType.DMA((8,)), pltpu.SemaphoreType.DMA((8,)),
                 pltpu.SemaphoreType.DMA((8,)), pltpu.SemaphoreType.DMA((8,)),
             ],
-            compiler_params=pltpu.CompilerParams(
-                collective_id=0, has_side_effects=True, vmem_limit_bytes=VMEM_GRANT
-            ),
+            compiler_params=pltpu.CompilerParams(collective_id=0, has_side_effects=True),
             name="pyramid",
         )(x)
         copies = sum(dims[1] for dims in tiled[:3])

time: 18.1 us -> 15.9 us (0.88)
  the two profiles are of different devices: /device:TPU:21 before, /device:TPU:0 now
where the time goes in v2:
time: 15.9 us; the launch traced here: 15.8 us
  Pallas kernels  15.2 us (96%)
  between operations  0.64 us (4%)
    pallas_call x1, Pallas kernels, body(): pl.pallas_call(functools.partial(kernel, image_cols), out_shape=tuple((vm...  13.5 us
    pallas_call x1, Pallas kernels, body(): pl.pallas_call(functools.partial(hand_out, f5), out_shape=tuple((shape(k)...  1.62 us

profile of v2, /device:TPU:0, one launch (start us, length us, event | category | flops | bytes accessed | tf_op | source)
XLA Modules:
  0.0 15.8 jit_solution(1018281343824481502)
XLA Ops:
  0.6 13.5 %pyramid.1 = (f32[3,4,128,128]{3,2,1,0:T(8,128)S(1)}, f32[3,2,64,128]{3,2,1,0:T(8,128)S(1)}, f32[3,1,32,128]{3,2,1,0:T(8,128)S(1)}, f32[3,1,16,128]{3,2,1,0:T(8,...) custom-call(f32[3,128,512]{2,1,0:T(8,128)} %x_hbm.1), custom_call_target="tpu_custom_call" | custom-call | tf_op jit(solution)/shard_map/pyramid/pallas_call | solution.py:355
  14.2 1.6 %hand_out.1 = (f32[3,128,512]{2,1,0:T(8,128)}, f32[3,64,256]{2,1,0:T(8,128)}, f32[3,32,128]{2,1,0:T(8,128)}, f32[3,16,64]{2,1,0:T(8,128)}, f32[3,8,32]{2,1,0:T(8,128)}, /*index=5*/f32[3,4,16]{2,1,0:T(4,128)}) custom-call(f32[3,4,128,128]{3,2,1,0:T(8,128)S(1)} %get-tuple-element.12.d0, f32[3,2,64,128]{3,2,1,0:T(8,128)S(1)} %get-tuple-element.13.d1, ...), custom_call_target="tpu_custom_call" | custom-call | tf_op jit(solution)/shard_map/hand_out/pallas_call | solution.py:387
